TPU v7x, 32 devices: a whole 2x2x4 slice. The times are simulated.
32 devices in a mesh: slab: 16 (over z, x, core), tile: 2 (over y).
Axes of the slice: x: 2, y: 2, z: 4, core: 2. Of those that a mesh axis runs over, the one named last changes fastest.
Arguments:
- features: bfloat16 [16, 2, 512, 128], P('slab', 'tile'), may hold values from -24 to 24
- counts: int32 [16, 2], P('slab', 'tile'), may hold values from 128 to 512, as said below
- rulebook: int32 [16, 2, 27, 512], P('slab', 'tile'), may hold values from 0 to 800, as said below
- face_rows: int32 [16, 2, 4, 64], P('slab', 'tile'), may hold values from 0 to 511, as said below
- conv_one: bfloat16 [27, 128, 128], replicated, may hold values from -0.109375 to 0.109375
- gain_one: float32 [128], replicated, may hold values from 0.5 to 1.5
- shift_one: float32 [128], replicated, may hold values from -0.5 to 0.5
- conv_two: bfloat16 [27, 128, 128], replicated, may hold values from -0.109375 to 0.109375
- gain_two: float32 [128], replicated, may hold values from 0.5 to 1.5
- shift_two: float32 [128], replicated, may hold values from -0.5 to 0.5
Outputs:
- output: bfloat16 [16, 2, 512, 128], P('slab', 'tile')
Inputs may be any that keep to these rules, and one draw needn't show every extreme that they name: `counts`: each device's voxels fill its 8 x 8 grid columns with the same number each, between 2 and 8; some device of the highest slab index holds 512. `rulebook`: an entry names the extended-table row that holds the voxel's neighbour at offset k = 9 (dx + 1) + 3 (dy + 1) + (dz + 1) of the submanifold 3x3x3 stencil, or 800 where that cell is inactive or outside the grid; the voxel itself is at offset 13; rows at or past the device's count name 800 at every offset. `face_rows`: lists 0 to 3 hold the device's voxels on its lower and higher face along the first, then the lower and higher face along the second dimension; the j-th voxel of the i-th column along a face stands at position i * 8 + j; unused positions name row 0.
All inputs are finite; a program needn't handle non-finite values.
Results may differ from a plain program's by a relative error of at most 0.0033.
Values may be sent and summed in bfloat16 or wider, within the bound.
A program may use at most 64 MiB of HBM per device.

v0:
```python
from functools import partial

import jax
import jax.numpy as jnp
from jax import lax
from jax.sharding import PartitionSpec as P

SIDE = 8


EPSILON = 1e-05


def extended(block, sides, width):
    for axis, dim in sides:
        count = lax.axis_size(axis)
        forward = [(i, i + 1) for i in range(count - 1)]
        backward = [(target, source) for source, target in forward]
        low = lax.ppermute(
            lax.slice_in_dim(block, block.shape[dim] - width, None, axis=dim), axis, forward
        )
        high = lax.ppermute(lax.slice_in_dim(block, 0, width, axis=dim), axis, backward)
        block = jnp.concatenate([low, block, high], axis=dim)
    return block


def build_table(local_rows, face_lists):
    face_len = face_lists.shape[1]
    column = face_len // SIDE
    picked = local_rows[face_lists]
    slab_recv = extended(picked[0:2], (("slab", 0),), 1)
    slab_low = slab_recv[0]
    slab_high = slab_recv[3]
    tile_send = jnp.stack(
        [
            jnp.concatenate([slab_low[:column], picked[2], slab_high[:column]], axis=0),
            jnp.concatenate(
                [slab_low[face_len - column :], picked[3], slab_high[face_len - column :]], axis=0
            ),
        ]
    )
    tile_recv = extended(tile_send, (("tile", 0),), 1)
    tile_low = tile_recv[0]
    tile_high = tile_recv[3]
    zero_row = jnp.zeros((1, local_rows.shape[1]), local_rows.dtype)
    return jnp.concatenate([local_rows, slab_low, slab_high, tile_low, tile_high, zero_row], axis=0)


def pick_rows(lookup, tap_index, offset, block_rows, flat_weight):
    gathered = jnp.take(lookup, tap_index.T, axis=0)
    gathered = gathered.reshape(block_rows, tap_index.shape[0] * lookup.shape[1])
    return jnp.dot(gathered, flat_weight, preferred_element_type=jnp.float32)


def convolve(lookup, tap_index, weight):
    total_rows = tap_index.shape[1]
    block_rows = min(512, total_rows)
    flat_weight = weight.reshape(weight.shape[0] * weight.shape[1], weight.shape[2])
    compute = partial(pick_rows, lookup, tap_index, 0, block_rows, flat_weight)
    result = compute()
    return result


def normalize(conv_out, live_mask, count_value, gain, shift):
    first_sum = jnp.sum(conv_out * live_mask, axis=0)
    square_sum = jnp.sum(conv_out * conv_out * live_mask, axis=0)
    channel_sums, square_sums, voxel_total = lax.psum(
        (first_sum, square_sum, count_value), ("slab", "tile")
    )
    average = channel_sums / voxel_total
    variance = square_sums / voxel_total - average * average
    return (conv_out - average) * lax.rsqrt(variance + EPSILON) * gain + shift


def per_device(
    features,
    counts,
    rulebook,
    face_rows,
    conv_one,
    gain_one,
    shift_one,
    conv_two,
    gain_two,
    shift_two,
):
    local_rows = features[0, 0]
    face_lists = face_rows[0, 0]
    tap_index = rulebook[0, 0]
    voxel_count = counts[0, 0]
    count_value = voxel_count.astype(jnp.float32)
    live_mask = (lax.broadcasted_iota(jnp.int32, (local_rows.shape[0], 1), 0) < voxel_count).astype(
        jnp.float32
    )
    first = convolve(build_table(local_rows, face_lists), tap_index, conv_one)
    hidden = (
        live_mask * jnp.maximum(normalize(first, live_mask, count_value, gain_one, shift_one), 0.0)
    ).astype(jnp.bfloat16)
    second = convolve(build_table(hidden, face_lists), tap_index, conv_two)
    summed = normalize(second, live_mask, count_value, gain_two, shift_two) + local_rows.astype(
        jnp.float32
    )
    output = (live_mask * jnp.maximum(summed, 0.0)).astype(jnp.bfloat16)
    return output[None, None]


def solution(mesh):
    placed = (
        P("slab", "tile", None, None),
        P("slab", "tile"),
        P("slab", "tile", None, None),
        P("slab", "tile", None, None),
        P(),
        P(),
        P(),
        P(),
        P(),
        P(),
    )
    return jax.shard_map(
        per_device,
        mesh=mesh,
        in_specs=placed,
        out_specs=P("slab", "tile", None, None),
        check_vma=False,
    )
```

profile of v0, /device:TPU:0, one launch (start us, length us, event | category | flops | bytes accessed | tf_op | source)
XLA Modules:
  0.0 215.5 jit_solution(16293700425668649573)
XLA Ops:
  0.0 0.0 copy-start
  0.0 0.8 compare_select_fusion.1
  0.8 0.1 reshape.78
  0.9 1.6 gather_fusion
  2.5 2.4 %collective-permute-start = (bf16[1,64,128]{2,1,0:T(8,128)(2,1)S(1)}, bf16[1,64,128]{2,1,0:T(8,128)(2,1)S(1)}, u32[]{:S(2)}, u32[]{:S(2)}) collective-permute-start(bf16[1,64,128]{2,1,0:T(8,128)(2,1)S(1)} %get-tuple-element.28), channel_id=1, source_target_pairs={{0,2},{2,4},{4,6},{6,8},{8,10},{10,12},{12,14},{14,16},{16,18},{18... | collective-permute-start | bytes 49160 | tf_op jit(solution)/shard_map/ppermute | solution.py:19
  4.9 1.3 collective-permute-start.1
  6.2 0.9 constant_dynamic-update-slice_fusion.5
  7.1 0.8 compare_select_fusion
  8.0 0.8 compare_and_fusion
  8.8 0.1 copy.15
  9.0 0.2 reshape.110
  9.9 0.2 copy.13
  10.0 0.0 collective-permute-done
  10.1 0.0 collective-permute-done.1
  10.1 4.2 %collective-permute-start.2 = (bf16[1,80,128]{2,1,0:T(8,128)(2,1)S(1)}, bf16[1,80,128]{2,1,0:T(8,128)(2,1)S(1)}, u32[]{:S(2)}, u32[]{:S(2)}) collective-permute-start(bf16[1,80,128]{2,1,0:T(8,128)(2,1)S(1)} %maximum_bitcast_fusion), channel_id=1, source_target_pairs={{0,1},{2,3},{4,5},{6,7},{8,9},{10,11},{12,13},{14,15},{16,17},{18,... | collective-permute-start | bytes 61448 | tf_op jit(solution)/shard_map/ppermute | solution.py:19
  14.4 1.3 collective-permute-start.3
  15.7 0.1 collective-permute-done.2
  15.8 4.2 %collective-permute-done.3 = bf16[1,80,128]{2,1,0:T(8,128)(2,1)S(1)} collective-permute-done((bf16[1,80,128]{2,1,0:T(8,128)(2,1)S(1)}, bf16[1,80,128]{2,1,0:T(8,128)(2,1)S(1)}, u32[]{:S(2)}, u32[]{:S(2)}) %collective-permute-start.3) | collective-permute-done | bytes 20512 | tf_op jit(solution)/shard_map/ppermute | solution.py:22
  20.1 28.6 %gather_fusion.2 = bf16[13824,128]{1,0:T(8,128)(2,1)} fusion(bf16[801,128]{1,0:T(8,128)(2,1)S(1)} %constant_dynamic-update-slice_fusion, s32[14336]{0:T(1024)S(1)} %pad_clamp_fusion), kind=kCustom, calls=%fused_computation.clone | custom fusion | bytes 7133184 | tf_op jit(solution)/shard_map/jit(_take)/gather | solution.py:50
  48.6 6.6 %reshape.113 = bf16[512,27,128]{2,1,0:T(8,128)(2,1)} reshape(bf16[13824,128]{1,0:T(8,128)(2,1)} %gather_fusion.2) | data formatting | bytes 7077888 | tf_op jit(solution)/shard_map/jit(_take)/gather | solution.py:50
  55.2 10.1 %broadcast_select_fusion = bf16[512,27,128]{2,1,0:T(8,128)(2,1)S(1)} fusion(bf16[512,27,128]{2,1,0:T(8,128)(2,1)} %reshape.113, pred[512,27]{1,0:T(8,128)(4,1)S(1)} %copy.13), kind=kLoop, calls=%fused_computation.4 | loop fusion | flops 1769472 | bytes 7091712 | tf_op jit(solution)/shard_map/jit(_take)/select_n | solution.py:50
  65.3 0.0 copy-done
  65.3 0.0 copy-start.2
  65.3 0.0 copy-start.3
  65.3 1.3 multiply_reduce_fusion.2
  66.6 42.9 %all-reduce.1 = (f32[128]{0:T(128)S(1)}, f32[]{:T(128)}, f32[128]{0:T(128)S(1)}) all-reduce(f32[128]{0:T(128)S(1)} %get-tuple-element.9, f32[]{:T(128)S(6)} %convert_element_type.21, f32[128]{0:T(128)S(1)} %get-tuple-element.8), channel_id=1, replica_groups=mesh['slab'=16,'tile'=2] {'slab','tile'}, use_global_device_ids=true, to_apply=%region_1.3 | all-reduce | flops 257 | bytes 2056 | tf_op jit(solution)/shard_map/psum | solution.py:67
  109.5 0.7 add_rsqrt_fusion.1
  110.2 0.0 copy-done.2
  110.2 0.0 copy-done.3
  110.2 0.1 constant_dynamic-update-slice_fusion.11
  110.4 0.9 gather_fusion.1
  111.2 1.3 collective-permute-start.4
  112.5 1.3 collective-permute-start.5
  113.8 0.0 collective-permute-done.4
  113.8 4.3 %collective-permute-done.5 = bf16[1,64,128]{2,1,0:T(8,128)(2,1)S(1)} collective-permute-done((bf16[1,64,128]{2,1,0:T(8,128)(2,1)S(1)}, bf16[1,64,128]{2,1,0:T(8,128)(2,1)S(1)}, u32[]{:S(2)}, u32[]{:S(2)}) %collective-permute-start.5) | collective-permute-done | bytes 16416 | tf_op jit(solution)/shard_map/ppermute | solution.py:22
  118.1 1.3 collective-permute-start.7
  119.4 4.5 %collective-permute-start.6 = (bf16[1,80,128]{2,1,0:T(8,128)(2,1)S(1)}, bf16[1,80,128]{2,1,0:T(8,128)(2,1)S(1)}, u32[]{:S(2)}, u32[]{:S(2)}) collective-permute-start(bf16[1,80,128]{2,1,0:T(8,128)(2,1)S(1)} %maximum_bitcast_fusion.2), channel_id=1, source_target_pairs={{0,1},{2,3},{4,5},{6,7},{8,9},{10,11},{12,13},{14,15},{16,17},{18,... | collective-permute-start | bytes 61448 | tf_op jit(solution)/shard_map/ppermute | solution.py:19
  124.0 1.4 collective-permute-done.6
  125.4 0.0 collective-permute-done.7
  125.5 28.6 %gather_fusion.3 = bf16[13824,128]{1,0:T(8,128)(2,1)} fusion(bf16[801,128]{1,0:T(8,128)(2,1)S(1)} %constant_dynamic-update-slice_fusion.6, s32[14336]{0:T(1024)S(1)} %pad_clamp_fusion), kind=kCustom, calls=%fused_computation.1.clone | custom fusion | bytes 7133184 | tf_op jit(solution)/shard_map/jit(_take)/gather | solution.py:50
  154.0 6.6 %reshape.117 = bf16[512,27,128]{2,1,0:T(8,128)(2,1)} reshape(bf16[13824,128]{1,0:T(8,128)(2,1)} %gather_fusion.3) | data formatting | bytes 7077888 | tf_op jit(solution)/shard_map/jit(_take)/gather | solution.py:50
  160.6 0.0 copy-start.6
  160.6 10.1 %broadcast_select_fusion.1 = bf16[512,27,128]{2,1,0:T(8,128)(2,1)S(1)} fusion(bf16[512,27,128]{2,1,0:T(8,128)(2,1)} %reshape.117, pred[512,27]{1,0:T(8,128)(4,1)S(1)} %copy.13), kind=kLoop, calls=%fused_computation.5 | loop fusion | flops 1769472 | bytes 7091712 | tf_op jit(solution)/shard_map/jit(_take)/select_n | solution.py:50
  170.8 0.0 copy-done.6
  170.8 0.0 copy-start.1
  170.8 0.0 copy-start.4
  170.8 0.0 copy-start.5
  170.8 1.2 multiply_reduce_fusion
  172.1 42.0 %all-reduce = (f32[128]{0:T(128)S(1)}, f32[128]{0:T(128)S(1)}) all-reduce(f32[128]{0:T(128)S(1)} %get-tuple-element.7, f32[128]{0:T(128)S(1)} %get-tuple-element.6), channel_id=1, replica_groups=mesh['slab'=16,'tile'=2] {'slab','tile'}, use_global_device_ids=true, to_apply=%region_6.8 | all-reduce | flops 256 | bytes 2048 | tf_op jit(solution)/shard_map/psum | solution.py:67
  214.1 0.7 add_rsqrt_fusion
  214.7 0.0 copy-done.1
  214.7 0.0 copy-done.4
  214.7 0.0 copy-done.5
  214.8 0.8 fusion.10
  (23 shorter events, 0.2 us)
Async XLA Ops:
  0.0 65.3 %copy-start = (bf16[27,128,128]{2,1,0:T(8,128)(2,1)S(1)}, bf16[27,128,128]{2,1,0:T(8,128)(2,1)}, u32[]{:S(2)}) copy-start(bf16[27,128,128]{2,1,0:T(8,128)(2,1)} %param.16) | copy-start | bytes 2654212
  2.5 7.5 %collective-permute-start = (bf16[1,64,128]{2,1,0:T(8,128)(2,1)S(1)}, bf16[1,64,128]{2,1,0:T(8,128)(2,1)S(1)}, u32[]{:S(2)}, u32[]{:S(2)}) collective-permute-start(bf16[1,64,128]{2,1,0:T(8,128)(2,1)S(1)} %get-tuple-element.28), channel_id=1, source_target_pairs={{0,2},{2,4},{4,6},{6,8},{8,10},{10,12},{12,14},{14,16},{16,18},{18... | collective-permute-start | bytes 49160 | tf_op jit(solution)/shard_map/ppermute | solution.py:19
  4.9 5.2 %collective-permute-start.1 = (bf16[1,64,128]{2,1,0:T(8,128)(2,1)S(1)}, bf16[1,64,128]{2,1,0:T(8,128)(2,1)S(1)}, u32[]{:S(2)}, u32[]{:S(2)}) collective-permute-start(bf16[1,64,128]{2,1,0:T(8,128)(2,1)S(1)} %get-tuple-element.27), channel_id=1, source_target_pairs={{2,0},{4,2},{6,4},{8,6},{10,8},{12,10},{14,12},{16,14},{18,16},{20... | collective-permute-start | bytes 49160 | tf_op jit(solution)/shard_map/ppermute | solution.py:22
  10.1 5.7 %collective-permute-start.2 = (bf16[1,80,128]{2,1,0:T(8,128)(2,1)S(1)}, bf16[1,80,128]{2,1,0:T(8,128)(2,1)S(1)}, u32[]{:S(2)}, u32[]{:S(2)}) collective-permute-start(bf16[1,80,128]{2,1,0:T(8,128)(2,1)S(1)} %maximum_bitcast_fusion), channel_id=1, source_target_pairs={{0,1},{2,3},{4,5},{6,7},{8,9},{10,11},{12,13},{14,15},{16,17},{18,... | collective-permute-start | bytes 61448 | tf_op jit(solution)/shard_map/ppermute | solution.py:19
  14.4 5.7 %collective-permute-start.3 = (bf16[1,80,128]{2,1,0:T(8,128)(2,1)S(1)}, bf16[1,80,128]{2,1,0:T(8,128)(2,1)S(1)}, u32[]{:S(2)}, u32[]{:S(2)}) collective-permute-start(bf16[1,80,128]{2,1,0:T(8,128)(2,1)S(1)} %maximum_bitcast_fusion.1), channel_id=1, source_target_pairs={{1,0},{3,2},{5,4},{7,6},{9,8},{11,10},{13,12},{15,14},{17,16},{19,... | collective-permute-start | bytes 61448 | tf_op jit(solution)/shard_map/ppermute | solution.py:22
  65.3 44.9 %copy-start.2 = (f32[128]{0:T(128)S(1)}, f32[128]{0:T(128)}, u32[]{:S(2)}) copy-start(f32[128]{0:T(128)} %param.18) | copy-start | bytes 1540
  65.3 44.9 %copy-start.3 = (f32[128]{0:T(128)S(1)}, f32[128]{0:T(128)}, u32[]{:S(2)}) copy-start(f32[128]{0:T(128)} %param.17) | copy-start | bytes 1540
  111.2 2.6 %collective-permute-start.4 = (bf16[1,64,128]{2,1,0:T(8,128)(2,1)S(1)}, bf16[1,64,128]{2,1,0:T(8,128)(2,1)S(1)}, u32[]{:S(2)}, u32[]{:S(2)}) collective-permute-start(bf16[1,64,128]{2,1,0:T(8,128)(2,1)S(1)} %get-tuple-element.24), channel_id=1, source_target_pairs={{0,2},{2,4},{4,6},{6,8},{8,10},{10,12},{12,14},{14,16},{16,18},{18... | collective-permute-start | bytes 49160 | tf_op jit(solution)/shard_map/ppermute | solution.py:19
  112.5 5.6 %collective-permute-start.5 = (bf16[1,64,128]{2,1,0:T(8,128)(2,1)S(1)}, bf16[1,64,128]{2,1,0:T(8,128)(2,1)S(1)}, u32[]{:S(2)}, u32[]{:S(2)}) collective-permute-start(bf16[1,64,128]{2,1,0:T(8,128)(2,1)S(1)} %get-tuple-element.23), channel_id=1, source_target_pairs={{2,0},{4,2},{6,4},{8,6},{10,8},{12,10},{14,12},{16,14},{18,16},{20... | collective-permute-start | bytes 49160 | tf_op jit(solution)/shard_map/ppermute | solution.py:22
  118.1 7.3 %collective-permute-start.7 = (bf16[1,80,128]{2,1,0:T(8,128)(2,1)S(1)}, bf16[1,80,128]{2,1,0:T(8,128)(2,1)S(1)}, u32[]{:S(2)}, u32[]{:S(2)}) collective-permute-start(bf16[1,80,128]{2,1,0:T(8,128)(2,1)S(1)} %maximum_bitcast_fusion.3), channel_id=1, source_target_pairs={{1,0},{3,2},{5,4},{7,6},{9,8},{11,10},{13,12},{15,14},{17,16},{19,... | collective-permute-start | bytes 61448 | tf_op jit(solution)/shard_map/ppermute | solution.py:22
  119.4 6.0 %collective-permute-start.6 = (bf16[1,80,128]{2,1,0:T(8,128)(2,1)S(1)}, bf16[1,80,128]{2,1,0:T(8,128)(2,1)S(1)}, u32[]{:S(2)}, u32[]{:S(2)}) collective-permute-start(bf16[1,80,128]{2,1,0:T(8,128)(2,1)S(1)} %maximum_bitcast_fusion.2), channel_id=1, source_target_pairs={{0,1},{2,3},{4,5},{6,7},{8,9},{10,11},{12,13},{14,15},{16,17},{18,... | collective-permute-start | bytes 61448 | tf_op jit(solution)/shard_map/ppermute | solution.py:19
  160.6 10.2 %copy-start.6 = (bf16[27,128,128]{2,1,0:T(8,128)(2,1)S(1)}, bf16[27,128,128]{2,1,0:T(8,128)(2,1)}, u32[]{:S(2)}) copy-start(bf16[27,128,128]{2,1,0:T(8,128)(2,1)} %param.19) | copy-start | bytes 2654212
  170.8 43.9 %copy-start.1 = (bf16[1,1,512,128]{3,2,1,0:T(8,128)(2,1)S(1)}, bf16[1,1,512,128]{3,2,1,0:T(8,128)(2,1)}, u32[]{:S(2)}) copy-start(bf16[1,1,512,128]{3,2,1,0:T(8,128)(2,1)} %param.12) | copy-start | bytes 393220
  170.8 43.9 %copy-start.4 = (f32[128]{0:T(128)S(1)}, f32[128]{0:T(128)}, u32[]{:S(2)}) copy-start(f32[128]{0:T(128)} %param.21) | copy-start | bytes 1540
  170.8 43.9 %copy-start.5 = (f32[128]{0:T(128)S(1)}, f32[128]{0:T(128)}, u32[]{:S(2)}) copy-start(f32[128]{0:T(128)} %param.20) | copy-start | bytes 1540
where the time goes:
time: 217 us; the launch traced here: 216 us
  blocking collectives  84.9 us (39%)
  local copies, waits for them, and re-layouts  74.5 us (34%)
  other arithmetic  24.9 us (11%)
  starting transfers between devices  17.6 us (8%)
  waiting for transfers between devices  10.1 us (5%)
  matrix products  2.55 us (1%)
    psum x2, blocking collectives, normalize(): lax.psum((first_sum, square_sum, count_value), ('slab', 'tile'))  84.9 us
    gather x4, local copies, waits for them, and re-layouts, pick_rows(): gathered = jnp.take(lookup, tap_index.T, axis=0)  70.3 us
    select_n x3, other arithmetic, pick_rows(): gathered = jnp.take(lookup, tap_index.T, axis=0)  21 us
    ppermute x4, starting transfers between devices, extended(): lax.ppermute(lax.slice_in_dim(block, block.shape[dim] - width, None, axis...  12.5 us
    ppermute x4, waiting for transfers between devices, extended(): lax.ppermute(lax.slice_in_dim(block, 0, width, axis=dim), axis, backward)  8.52 us
    ppermute x4, starting transfers between devices, extended(): lax.ppermute(lax.slice_in_dim(block, 0, width, axis=dim), axis, backward)  5.16 us
  transfers between devices with their start and end apart: 8, of which 4 were waited for; matrix products, arithmetic and copies ran while one was open for 1% of the time, Pallas kernels for 0%

commit v1 on v0

v1 whole, which is shorter than its diff:
```python
from functools import partial

import jax
import jax.numpy as jnp
from jax import lax
from jax.experimental import pallas as pl
from jax.experimental.pallas import tpu as pltpu
from jax.sharding import PartitionSpec as P

SIDE = 8
EPSILON = 1e-05
MESH = pl.DeviceIdType.MESH
BLOCK = 256
PIECE = 16
F32 = jnp.float32
BF16 = jnp.bfloat16


def transfers(face_len):
    low, high = 0, face_len
    edge = face_len - PIECE
    end = PIECE + face_len
    return (
        (1, 0, high, face_len, 0, 0),
        (-1, 0, low, face_len, 0, face_len),
        (0, 1, 3 * face_len, face_len, 1, PIECE),
        (0, -1, 2 * face_len, face_len, 2, PIECE),
        (1, 1, high + edge, PIECE, 1, 0),
        (-1, 1, low + edge, PIECE, 1, end),
        (1, -1, high, PIECE, 2, 0),
        (-1, -1, low, PIECE, 2, end),
    )


def block_kernel(
    n_slab,
    n_tile,
    feat_ref,
    count_ref,
    rule_ref,
    face_ref,
    gain_one_ref,
    shift_one_ref,
    gain_two_ref,
    shift_two_ref,
    conv_one_ref,
    conv_two_ref,
    out_ref,
    weight_ref,
    weight_t_ref,
    onehot_ref,
    part_ref,
    face_hot_ref,
    square_ref,
    send_ref,
    halo_ref,
    lhs_ref,
    picked_ref,
    stats_ref,
    weight_sem,
    send_sem,
    recv_sem,
    stat_send_sem,
    stat_recv_sem,
):
    rows, channels = feat_ref.shape
    taps = rule_ref.shape[0]
    face_len = face_ref.shape[1]
    column = face_len // SIDE
    n_dev = n_slab * n_tile
    blocks = rows // BLOCK
    group = taps // 3
    slab = lax.axis_index("slab")
    tile = lax.axis_index("tile")
    me = slab * n_tile + tile

    weight_copies = [
        pltpu.make_async_copy(src, weight_ref.at[i], weight_sem.at[i])
        for i, src in enumerate((conv_one_ref, conv_two_ref))
    ]
    for copy in weight_copies:
        copy.start()
    halo_ref[...] = jnp.zeros_like(halo_ref)

    def peer_of(step):
        peer = lax.rem(me + step, n_dev)
        return {"slab": peer // n_tile, "tile": lax.rem(peer, n_tile)}

    barrier = pltpu.get_barrier_semaphore()

    def greet(step, carry):
        pl.semaphore_signal(barrier, inc=1, device_id=peer_of(step), device_id_type=MESH)
        return carry

    lax.fori_loop(1, n_dev, greet, 0)

    def halo(which, start):
        for j, (ds, dt, first, size, buffer, place) in enumerate(transfers(face_len)):
            copy = pltpu.make_async_remote_copy(
                src_ref=send_ref.at[which, pl.ds(first, size)],
                dst_ref=halo_ref.at[which, buffer, pl.ds(place, size)],
                send_sem=send_sem.at[which, j],
                recv_sem=recv_sem.at[which, j],
                device_id={"slab": slab + ds, "tile": tile + dt},
                device_id_type=MESH,
            )
            sends, receives = True, True
            if ds > 0:
                sends, receives = slab < n_slab - 1, slab > 0
            elif ds < 0:
                sends, receives = slab > 0, slab < n_slab - 1
            if dt > 0:
                sends, receives = sends & (tile < n_tile - 1), receives & (tile > 0)
            elif dt < 0:
                sends, receives = sends & (tile > 0), receives & (tile < n_tile - 1)
            if start:
                pl.when(sends)(copy.start)
            else:
                pl.when(receives)(copy.wait_recv)
                pl.when(sends)(copy.wait_send)

    square_ref[...] = jnp.zeros_like(square_ref)
    square_ref[0:4, 0:face_len] = face_ref[...].astype(F32)
    face_cols = square_ref[...].T
    lane_rows = lax.broadcasted_iota(jnp.int32, (face_len, rows), 1)
    for k in range(4):
        wanted = face_cols[0:face_len, k : k + 1].astype(jnp.int32)
        face_hot_ref[k * face_len : (k + 1) * face_len, :] = jnp.where(
            lane_rows == wanted, 1.0, 0.0
        ).astype(BF16)

    feat = feat_ref[...]
    send_ref[0] = jnp.dot(face_hot_ref[...], feat, preferred_element_type=F32).astype(BF16)
    pl.semaphore_wait(barrier, n_dev - 1)
    halo(0, True)

    rule = rule_ref[...]
    tile_len = face_len + 2 * column
    below = rows + 2 * face_len
    above = below + tile_len
    q_low = rule - below
    q_high = rule - above
    base = 2 * face_len + PIECE - column
    skip = PIECE - column
    place_low = base + q_low + jnp.where(q_low >= column + face_len, skip, 0)
    place_high = base + q_high - jnp.where(q_high < column, skip, 0)
    place = jnp.where(
        rule < rows,
        rule & (BLOCK - 1),
        jnp.where(
            rule < below, rule - rows, jnp.where(rule < above, place_low, place_high)
        ),
    )
    part = jnp.where(
        rule < rows, rule // BLOCK, jnp.where(rule < above + tile_len, blocks, blocks + 1)
    )
    position = lax.broadcasted_iota(jnp.int32, (BLOCK, rows), 0)
    for k in range(taps):
        part_ref[k] = part[k : k + 1]
        onehot_ref[k] = jnp.where(position == place[k : k + 1], 1.0, 0.0).astype(BF16)

    def load_local(values):
        for b in range(blocks):
            turned = values[b * BLOCK : (b + 1) * BLOCK].T
            for y in range(3):
                lhs_ref[y, b * channels : (b + 1) * channels, :] = turned

    def load_halo(which):
        turned = [halo_ref[which, i].T for i in range(3)]
        low = blocks * channels
        half = BLOCK // 2
        for y, other in ((0, turned[1]), (1, None), (2, turned[2])):
            lhs_ref[y, low:, 0:half] = turned[0]
            lhs_ref[y, low:, half:] = jnp.zeros_like(turned[0]) if other is None else other

    load_local(feat)
    for i in range(2):
        weight_copies[i].wait()
        for x in range(3):
            weight_t_ref[i, x] = weight_ref[i, x * group * channels : (x + 1) * group * channels, :].T

    def convolve(which):
        def one(x, total):
            for j in range(group):
                tap = x * group + j
                found = jnp.dot(
                    lhs_ref[j // 3], onehot_ref[tap], preferred_element_type=F32
                )
                home = part_ref[tap]
                value = jnp.zeros((channels, rows), F32)
                for b in range(blocks + 1):
                    value = jnp.where(
                        home == b, found[b * channels : (b + 1) * channels], value
                    )
                picked_ref[j * channels : (j + 1) * channels, :] = value.astype(BF16)
            return total + jnp.dot(
                weight_t_ref[which, x], picked_ref[...], preferred_element_type=F32
            )

        return lax.fori_loop(0, 3, one, jnp.zeros((channels, rows), F32))

    count = count_ref[0, 0]
    live = (lax.broadcasted_iota(jnp.int32, (rows, 1), 0) < count).astype(F32)

    def stat_copy(which, target):
        return pltpu.make_async_remote_copy(
            src_ref=stats_ref.at[which, me],
            dst_ref=stats_ref.at[which, me],
            send_sem=stat_send_sem.at[which],
            recv_sem=stat_recv_sem.at[which],
            device_id=target,
            device_id_type=MESH,
        )

    def affine(which, values, gain_ref, shift_ref):
        kept = values * live
        stats_ref[which, me] = jnp.concatenate(
            [
                jnp.sum(kept, axis=0, keepdims=True),
                jnp.sum(kept * values, axis=0, keepdims=True),
                jnp.full((2, channels), count.astype(F32)),
            ],
            axis=0,
        )

        def tell(step, carry):
            stat_copy(which, peer_of(step)).start()
            return carry

        lax.fori_loop(1, n_dev, tell, 0)
        others = stats_ref.at[which, pl.ds(0, n_dev - 1)]
        pltpu.make_async_copy(others, others, stat_recv_sem.at[which]).wait()
        pltpu.make_async_copy(others, others, stat_send_sem.at[which]).wait()
        total = jnp.sum(stats_ref[which], axis=0)
        average = total[0:1] / total[2:3]
        variance = total[1:2] / total[2:3] - average * average
        scale = lax.rsqrt(variance + EPSILON) * gain_ref[...]
        return (values - average) * scale + shift_ref[...]

    halo(0, False)
    load_halo(0)
    first = convolve(0).T
    hidden = (live * jnp.maximum(affine(0, first, gain_one_ref, shift_one_ref), 0.0)).astype(BF16)
    send_ref[1] = jnp.dot(face_hot_ref[...], hidden, preferred_element_type=F32).astype(BF16)
    halo(1, True)
    load_local(hidden)
    halo(1, False)
    load_halo(1)
    second = convolve(1).T
    summed = affine(1, second, gain_two_ref, shift_two_ref) + feat.astype(F32)
    out_ref[...] = (live * jnp.maximum(summed, 0.0)).astype(BF16)


def per_device(
    n_slab,
    n_tile,
    features,
    counts,
    rulebook,
    face_rows,
    conv_one,
    gain_one,
    shift_one,
    conv_two,
    gain_two,
    shift_two,
):
    rows, channels = features.shape[2:]
    taps = rulebook.shape[2]
    faces, face_len = face_rows.shape[2:]
    blocks = rows // BLOCK
    vmem = pl.BlockSpec(memory_space=pltpu.VMEM)
    smem = pl.BlockSpec(memory_space=pltpu.SMEM)
    hbm = pl.BlockSpec(memory_space=pl.ANY)
    group = taps // 3 * channels
    output = pl.pallas_call(
        partial(block_kernel, n_slab, n_tile),
        out_shape=jax.ShapeDtypeStruct((rows, channels), features.dtype),
        in_specs=[vmem, smem, vmem, vmem, vmem, vmem, vmem, vmem, hbm, hbm],
        out_specs=vmem,
        scratch_shapes=[
            pltpu.VMEM((2, taps * channels, channels), BF16),
            pltpu.VMEM((2, 3, channels, group), BF16),
            pltpu.VMEM((taps, BLOCK, rows), BF16),
            pltpu.VMEM((taps, 1, rows), jnp.int32),
            pltpu.VMEM((faces * face_len, rows), BF16),
            pltpu.VMEM((128, 128), F32),
            pltpu.VMEM((2, faces * face_len, channels), BF16),
            pltpu.VMEM((2, 3, BLOCK // 2, channels), BF16),
            pltpu.VMEM((3, (blocks + 1) * channels, BLOCK), BF16),
            pltpu.VMEM((group, rows), BF16),
            pltpu.VMEM((2, n_slab * n_tile, 4, channels), F32),
            pltpu.SemaphoreType.DMA((2,)),
            pltpu.SemaphoreType.DMA((2, 8)),
            pltpu.SemaphoreType.DMA((2, 8)),
            pltpu.SemaphoreType.DMA((2,)),
            pltpu.SemaphoreType.DMA((2,)),
        ],
        compiler_params=pltpu.CompilerParams(
            collective_id=0, has_side_effects=True, vmem_limit_bytes=50 * 1024 * 1024
        ),
    )(
        features[0, 0],
        counts,
        rulebook[0, 0],
        face_rows[0, 0],
        gain_one[None],
        shift_one[None],
        gain_two[None],
        shift_two[None],
        conv_one.reshape(taps * channels, channels),
        conv_two.reshape(taps * channels, channels),
    )
    return output[None, None]


def solution(mesh):
    placed = (
        P("slab", "tile", None, None),
        P("slab", "tile"),
        P("slab", "tile", None, None),
        P("slab", "tile", None, None),
        P(),
        P(),
        P(),
        P(),
        P(),
        P(),
    )
    return jax.shard_map(
        partial(per_device, mesh.shape["slab"], mesh.shape["tile"]),
        mesh=mesh,
        in_specs=placed,
        out_specs=P("slab", "tile", None, None),
        check_vma=False,
    )
```

time: 217 us -> 37.1 us (0.17)
  blocking collectives: 84.9 us -> 0 us
  local copies, waits for them, and re-layouts: 74.5 us -> 4.48 us
  Pallas kernels: 0 us -> 31.6 us
  other arithmetic: 24.9 us -> 0 us
  starting transfers between devices: 17.6 us -> 0 us
  waiting for transfers between devices: 10.1 us -> 0 us
  matrix products: 2.55 us -> 0 us
    psum x2 -> x0, blocking collectives: 84.9 us -> none  [normalize(): lax.psum((first_sum, square_sum, count_value), ('slab', 'tile'))]
    gather x6 -> x0, local copies, waits for them, and re-layouts: 72.8 us -> none  [the longest x4 70.3 us: pick_rows(): gathered = jnp.take(lookup, tap_index.T, axis=0)]
    pallas_call x0 -> x1, Pallas kernels: none -> 31.6 us  [per_device(): pl.pallas_call(partial(block_kernel, n_slab, n_tile), out_shape=jax.Shape...]
    select_n x4 -> x0, other arithmetic: 21.8 us -> none  [the longest x3 21 us: pick_rows(): gathered = jnp.take(lookup, tap_index.T, axis=0)]
    ppermute x8 -> x0, starting transfers between devices: 17.6 us -> none  [the longest x4 12.5 us: extended(): lax.ppermute(lax.slice_in_dim(block, block.shape[dim] - width, None, axis...]
    ppermute x8 -> x0, waiting for transfers between devices: 10.1 us -> none  [the longest x4 8.52 us: extended(): lax.ppermute(lax.slice_in_dim(block, 0, width, axis=dim), axis, backward)]
    unnamed x23 -> x18, local copies, waits for them, and re-layouts: 1.03 us -> 4.48 us
    dot_general x2 -> x0, matrix products: 2.55 us -> none  [pick_rows(): return jnp.dot(gathered, flat_weight, preferred_element_type=jnp.float32)]
  transfers between devices with their start and end apart: 8 -> 0, of which waited for: 4 -> 0; matrix products, arithmetic and copies ran while one was open for 1% -> 0% of each run, Pallas kernels for 0% -> 0%
where the time goes in v1:
time: 37.1 us; the launch traced here: 36.8 us
  Pallas kernels  31.6 us (85%)
  local copies, waits for them, and re-layouts  4.48 us (12%)
  between operations  0.75 us (2%)
    pallas_call x1, Pallas kernels, per_device(): pl.pallas_call(partial(block_kernel, n_slab, n_tile), out_shape=jax.Shape...  31.6 us
    unnamed x18, local copies, waits for them, and re-layouts  4.48 us

profile of v1, /device:TPU:0, one launch (start us, length us, event | category | flops | bytes accessed | tf_op | source)
XLA Modules:
  0.0 36.8 jit_solution(14219090534992722218)
XLA Ops:
  0.0 0.0 copy-start.2
  0.7 0.0 copy-start.3
  0.7 0.0 copy-start.7
  0.7 0.8 %copy.13 = s32[1,1,27,512]{3,2,1,0:T(8,128)S(1)} copy(s32[1,1,27,512]{3,1,2,0:T(1,128)} %param.12) | data formatting | bytes 110592
  1.5 0.0 copy-start.4
  1.5 0.0 copy-start.5
  1.5 0.0 copy-start.6
  1.6 0.0 copy-done.2
  1.6 0.0 copy-done.3
  1.6 0.0 copy-done.7
  1.6 0.6 %copy-done.4 = f32[128]{0:T(128)S(1)} copy-done((f32[128]{0:T(128)S(1)}, f32[128]{0:T(128)}, u32[]{:S(2)}) %copy-start.4) | copy-done | bytes 536
  2.2 0.0 copy-done.5
  2.2 0.0 copy-done.6
  2.2 0.0 copy-start
  2.2 1.2 %copy-done = bf16[27,128,128]{2,1,0:T(8,128)(2,1)S(1)} copy-done((bf16[27,128,128]{2,1,0:T(8,128)(2,1)S(1)}, bf16[27,128,128]{2,1,0:T(8,128)(2,1)}, u32[]{:S(2)}) %copy-start) | copy-done | bytes 884760
  3.4 0.0 copy-start.1
  3.4 1.2 %copy-done.1 = bf16[27,128,128]{2,1,0:T(8,128)(2,1)S(1)} copy-done((bf16[27,128,128]{2,1,0:T(8,128)(2,1)S(1)}, bf16[27,128,128]{2,1,0:T(8,128)(2,1)}, u32[]{:S(2)}) %copy-start.1) | copy-done | bytes 884760
  4.6 31.6 %shard_map.100 = bf16[512,128]{1,0:T(8,128)(2,1)S(1)} custom-call(bf16[512,128]{1,0:T(8,128)(2,1)S(1)} %bitcast.16, s32[1,1]{1,0:T(1,128)S(6)} %copy.15.count_ref, s32[27,512]{1,0:T(8,128)S(1)} %bitcast.15, s32[4,64]{1,0:T(4,128)S(1)} %bitcast.17, f32[1,128]{1,0:T(1,128)S(1)} %bitcast.18, f32[1,128]{1,0:T(1,128)S(1)} %bitcast.19, f32[1,128]{1,0:T(1,128)S(1)} %bitcast.20, ...), custom_call_target="tpu_custom_call" | custom-call | tf_op jit(solution)/shard_map/pallas_call | solution.py:276
  36.1 0.7 %copy.16 = bf16[1,1,512,128]{3,2,1,0:T(8,128)(2,1)} copy(bf16[1,1,512,128]{3,2,1,0:T(8,128)(2,1)S(1)} %bitcast.14) | data formatting | bytes 262144
Async XLA Ops:
  0.0 1.6 %copy-start.2 = (bf16[1,1,512,128]{3,2,1,0:T(8,128)(2,1)S(1)}, bf16[1,1,512,128]{3,2,1,0:T(8,128)(2,1)}, u32[]{:S(2)}) copy-start(bf16[1,1,512,128]{3,2,1,0:T(8,128)(2,1)} %param.10) | copy-start | bytes 393220
  0.7 0.9 %copy-start.3 = (s32[1,1,4,64]{3,2,1,0:T(4,128)S(1)}, s32[1,1,4,64]{3,2,1,0:T(4,128)}, u32[]{:S(2)}) copy-start(s32[1,1,4,64]{3,2,1,0:T(4,128)} %param.13) | copy-start | bytes 3076
  0.7 0.9 %copy-start.7 = (f32[128]{0:T(128)S(1)}, f32[128]{0:T(128)}, u32[]{:S(2)}) copy-start(f32[128]{0:T(128)} %param.19) | copy-start | bytes 1540
  1.5 0.7 %copy-start.4 = (f32[128]{0:T(128)S(1)}, f32[128]{0:T(128)}, u32[]{:S(2)}) copy-start(f32[128]{0:T(128)} %param.15) | copy-start | bytes 1540
  1.5 0.7 %copy-start.5 = (f32[128]{0:T(128)S(1)}, f32[128]{0:T(128)}, u32[]{:S(2)}) copy-start(f32[128]{0:T(128)} %param.16) | copy-start | bytes 1540
  1.5 0.7 %copy-start.6 = (f32[128]{0:T(128)S(1)}, f32[128]{0:T(128)}, u32[]{:S(2)}) copy-start(f32[128]{0:T(128)} %param.18) | copy-start | bytes 1540
  2.2 1.2 %copy-start = (bf16[27,128,128]{2,1,0:T(8,128)(2,1)S(1)}, bf16[27,128,128]{2,1,0:T(8,128)(2,1)}, u32[]{:S(2)}) copy-start(bf16[27,128,128]{2,1,0:T(8,128)(2,1)} %param.14) | copy-start | bytes 2654212
  3.4 1.2 %copy-start.1 = (bf16[27,128,128]{2,1,0:T(8,128)(2,1)S(1)}, bf16[27,128,128]{2,1,0:T(8,128)(2,1)}, u32[]{:S(2)}) copy-start(bf16[27,128,128]{2,1,0:T(8,128)(2,1)} %param.17) | copy-start | bytes 2654212

commit v2 on v1

--- a/solution.py
+++ b/solution.py
@@ -35,10 +35,10 @@
 def block_kernel(
     n_slab,
     n_tile,
-    feat_ref,
+    feat_hbm,
     count_ref,
-    rule_ref,
-    face_ref,
+    rule_hbm,
+    face_hbm,
     gain_one_ref,
     shift_one_ref,
     gain_two_ref,
@@ -46,6 +46,9 @@
     conv_one_ref,
     conv_two_ref,
     out_ref,
+    feat_ref,
+    rule_ref,
+    face_ref,
     weight_ref,
     weight_t_ref,
     onehot_ref,
@@ -53,10 +56,13 @@
     face_hot_ref,
     square_ref,
     send_ref,
+    wide_send_ref,
     halo_ref,
+    wide_halo_ref,
     lhs_ref,
     picked_ref,
     stats_ref,
+    input_sem,
     weight_sem,
     send_sem,
     recv_sem,
@@ -74,6 +80,14 @@
     tile = lax.axis_index("tile")
     me = slab * n_tile + tile
 
+    input_copies = [
+        pltpu.make_async_copy(src, dst, input_sem.at[i])
+        for i, (src, dst) in enumerate(
+            ((feat_hbm, feat_ref), (face_hbm, face_ref), (rule_hbm, rule_ref))
+        )
+    ]
+    for copy in input_copies:
+        copy.start()
     weight_copies = [
         pltpu.make_async_copy(src, weight_ref.at[i], weight_sem.at[i])
         for i, src in enumerate((conv_one_ref, conv_two_ref))
@@ -81,6 +95,7 @@
     for copy in weight_copies:
         copy.start()
     halo_ref[...] = jnp.zeros_like(halo_ref)
+    wide_halo_ref[...] = jnp.zeros_like(wide_halo_ref)
 
     def peer_of(step):
         peer = lax.rem(me + step, n_dev)
@@ -95,10 +110,11 @@
     lax.fori_loop(1, n_dev, greet, 0)
 
     def halo(which, start):
+        source, target = ((send_ref, halo_ref), (wide_send_ref, wide_halo_ref))[which]
         for j, (ds, dt, first, size, buffer, place) in enumerate(transfers(face_len)):
             copy = pltpu.make_async_remote_copy(
-                src_ref=send_ref.at[which, pl.ds(first, size)],
-                dst_ref=halo_ref.at[which, buffer, pl.ds(place, size)],
+                src_ref=source.at[pl.ds(first, size)],
+                dst_ref=target.at[buffer, pl.ds(place, size)],
                 send_sem=send_sem.at[which, j],
                 recv_sem=recv_sem.at[which, j],
                 device_id={"slab": slab + ds, "tile": tile + dt},
@@ -119,6 +135,7 @@
                 pl.when(receives)(copy.wait_recv)
                 pl.when(sends)(copy.wait_send)
 
+    input_copies[1].wait()
     square_ref[...] = jnp.zeros_like(square_ref)
     square_ref[0:4, 0:face_len] = face_ref[...].astype(F32)
     face_cols = square_ref[...].T
@@ -129,11 +146,11 @@
             lane_rows == wanted, 1.0, 0.0
         ).astype(BF16)
 
+    input_copies[0].wait()
     feat = feat_ref[...]
-    send_ref[0] = jnp.dot(face_hot_ref[...], feat, preferred_element_type=F32).astype(BF16)
-    pl.semaphore_wait(barrier, n_dev - 1)
-    halo(0, True)
-
+    send_ref[...] = jnp.dot(face_hot_ref[...], feat, preferred_element_type=F32).astype(BF16)
+
+    input_copies[2].wait()
     rule = rule_ref[...]
     tile_len = face_len + 2 * column
     below = rows + 2 * face_len
@@ -154,10 +171,13 @@
     part = jnp.where(
         rule < rows, rule // BLOCK, jnp.where(rule < above + tile_len, blocks, blocks + 1)
     )
+    part_ref[...] = part
     position = lax.broadcasted_iota(jnp.int32, (BLOCK, rows), 0)
     for k in range(taps):
-        part_ref[k] = part[k : k + 1]
-        onehot_ref[k] = jnp.where(position == place[k : k + 1], 1.0, 0.0).astype(BF16)
+        onehot_ref[k] = jnp.where(position == place[k], 1.0, 0.0).astype(BF16)
+
+    pl.semaphore_wait(barrier, n_dev - 1)
+    halo(0, True)
 
     def load_local(values):
         for b in range(blocks):
@@ -165,8 +185,8 @@
             for y in range(3):
                 lhs_ref[y, b * channels : (b + 1) * channels, :] = turned
 
-    def load_halo(which):
-        turned = [halo_ref[which, i].T for i in range(3)]
+    def load_halo(pieces):
+        turned = [piece.T for piece in pieces]
         low = blocks * channels
         half = BLOCK // 2
         for y, other in ((0, turned[1]), (1, None), (2, turned[2])):
@@ -179,23 +199,41 @@
         for x in range(3):
             weight_t_ref[i, x] = weight_ref[i, x * group * channels : (x + 1) * group * channels, :].T
 
-    def convolve(which):
+    def choose(home, found, value, chosen):
+        for i, b in enumerate(chosen):
+            value = jnp.where(home == b, found[i * channels : (i + 1) * channels], value)
+        return value
+
+    def pick_local(tap, carry):
+        found = jnp.dot(
+            lhs_ref[0, 0 : blocks * channels], onehot_ref[tap], preferred_element_type=F32
+        )
+        value = choose(part_ref[tap], found, jnp.zeros((channels, rows), F32), range(blocks))
+        picked_ref[tap] = value.astype(BF16)
+        return carry
+
+    def convolve(which, picked):
         def one(x, total):
             for j in range(group):
                 tap = x * group + j
-                found = jnp.dot(
-                    lhs_ref[j // 3], onehot_ref[tap], preferred_element_type=F32
-                )
                 home = part_ref[tap]
-                value = jnp.zeros((channels, rows), F32)
-                for b in range(blocks + 1):
-                    value = jnp.where(
-                        home == b, found[b * channels : (b + 1) * channels], value
+                if picked:
+                    found = jnp.dot(
+                        lhs_ref[j // 3, blocks * channels :],
+                        onehot_ref[tap],
+                        preferred_element_type=F32,
                     )
-                picked_ref[j * channels : (j + 1) * channels, :] = value.astype(BF16)
-            return total + jnp.dot(
-                weight_t_ref[which, x], picked_ref[...], preferred_element_type=F32
-            )
+                    value = choose(home, found, picked_ref[tap].astype(F32), (blocks,))
+                else:
+                    found = jnp.dot(
+                        lhs_ref[j // 3], onehot_ref[tap], preferred_element_type=F32
+                    )
+                    value = choose(
+                        home, found, jnp.zeros((channels, rows), F32), range(blocks + 1)
+                    )
+                picked_ref[tap] = value.astype(BF16)
+            taken = picked_ref[pl.ds(x * group, group)].reshape(group * channels, rows)
+            return total + jnp.dot(weight_t_ref[which, x], taken, preferred_element_type=F32)
 
         return lax.fori_loop(0, 3, one, jnp.zeros((channels, rows), F32))
 
@@ -212,7 +250,7 @@
             device_id_type=MESH,
         )
 
-    def affine(which, values, gain_ref, shift_ref):
+    def tell_sums(which, values):
         kept = values * live
         stats_ref[which, me] = jnp.concatenate(
             [
@@ -228,6 +266,8 @@
             return carry
 
         lax.fori_loop(1, n_dev, tell, 0)
+
+    def affine(which, gain_ref, shift_ref):
         others = stats_ref.at[which, pl.ds(0, n_dev - 1)]
         pltpu.make_async_copy(others, others, stat_recv_sem.at[which]).wait()
         pltpu.make_async_copy(others, others, stat_send_sem.at[which]).wait()
@@ -235,19 +275,30 @@
         average = total[0:1] / total[2:3]
         variance = total[1:2] / total[2:3] - average * average
         scale = lax.rsqrt(variance + EPSILON) * gain_ref[...]
-        return (values - average) * scale + shift_ref[...]
-
+        return lambda values: (values - average) * scale + shift_ref[...]
+
+    lax.fori_loop(0, taps, pick_local, 0, unroll=3)
     halo(0, False)
-    load_halo(0)
-    first = convolve(0).T
-    hidden = (live * jnp.maximum(affine(0, first, gain_one_ref, shift_one_ref), 0.0)).astype(BF16)
-    send_ref[1] = jnp.dot(face_hot_ref[...], hidden, preferred_element_type=F32).astype(BF16)
+    load_halo([halo_ref[i] for i in range(3)])
+    first = convolve(0, True).T
+    tell_sums(0, first)
+    coarse = first.astype(BF16)
+    fine = (first - coarse.astype(F32)).astype(BF16)
+    both = jnp.dot(
+        face_hot_ref[...],
+        jnp.concatenate([coarse, fine], axis=1),
+        preferred_element_type=F32,
+    )
+    wide_send_ref[...] = both[:, 0:channels] + both[:, channels:]
     halo(1, True)
-    load_local(hidden)
+    norm_one = affine(0, gain_one_ref, shift_one_ref)
+    load_local((live * jnp.maximum(norm_one(first), 0.0)).astype(BF16))
     halo(1, False)
-    load_halo(1)
-    second = convolve(1).T
-    summed = affine(1, second, gain_two_ref, shift_two_ref) + feat.astype(F32)
+    load_halo([jnp.maximum(norm_one(wide_halo_ref[i]), 0.0).astype(BF16) for i in range(3)])
+    second = convolve(1, False).T
+    tell_sums(1, second)
+    norm_two = affine(1, gain_two_ref, shift_two_ref)
+    summed = norm_two(second) + feat_ref[...].astype(F32)
     out_ref[...] = (live * jnp.maximum(summed, 0.0)).astype(BF16)
 
 
@@ -269,27 +320,33 @@
     taps = rulebook.shape[2]
     faces, face_len = face_rows.shape[2:]
     blocks = rows // BLOCK
+    smem = pl.BlockSpec(memory_space=pltpu.SMEM)
     vmem = pl.BlockSpec(memory_space=pltpu.VMEM)
-    smem = pl.BlockSpec(memory_space=pltpu.SMEM)
-    hbm = pl.BlockSpec(memory_space=pl.ANY)
+    hbm = pl.BlockSpec(memory_space=pltpu.HBM)
     group = taps // 3 * channels
     output = pl.pallas_call(
         partial(block_kernel, n_slab, n_tile),
         out_shape=jax.ShapeDtypeStruct((rows, channels), features.dtype),
-        in_specs=[vmem, smem, vmem, vmem, vmem, vmem, vmem, vmem, hbm, hbm],
+        in_specs=[hbm, smem, hbm, hbm, vmem, vmem, vmem, vmem, hbm, hbm],
         out_specs=vmem,
         scratch_shapes=[
+            pltpu.VMEM((rows, channels), BF16),
+            pltpu.VMEM((taps, 1, rows), jnp.int32),
+            pltpu.VMEM((faces, face_len), jnp.int32),
             pltpu.VMEM((2, taps * channels, channels), BF16),
             pltpu.VMEM((2, 3, channels, group), BF16),
             pltpu.VMEM((taps, BLOCK, rows), BF16),
             pltpu.VMEM((taps, 1, rows), jnp.int32),
             pltpu.VMEM((faces * face_len, rows), BF16),
             pltpu.VMEM((128, 128), F32),
-            pltpu.VMEM((2, faces * face_len, channels), BF16),
-            pltpu.VMEM((2, 3, BLOCK // 2, channels), BF16),
+            pltpu.VMEM((faces * face_len, channels), BF16),
+            pltpu.VMEM((faces * face_len, channels), F32),
+            pltpu.VMEM((3, BLOCK // 2, channels), BF16),
+            pltpu.VMEM((3, BLOCK // 2, channels), F32),
             pltpu.VMEM((3, (blocks + 1) * channels, BLOCK), BF16),
-            pltpu.VMEM((group, rows), BF16),
+            pltpu.VMEM((taps, channels, rows), BF16),
             pltpu.VMEM((2, n_slab * n_tile, 4, channels), F32),
+            pltpu.SemaphoreType.DMA((3,)),
             pltpu.SemaphoreType.DMA((2,)),
             pltpu.SemaphoreType.DMA((2, 8)),
             pltpu.SemaphoreType.DMA((2, 8)),
@@ -297,12 +354,12 @@
             pltpu.SemaphoreType.DMA((2,)),
         ],
         compiler_params=pltpu.CompilerParams(
-            collective_id=0, has_side_effects=True, vmem_limit_bytes=50 * 1024 * 1024
+            collective_id=0, has_side_effects=True, vmem_limit_bytes=55500000
         ),
     )(
         features[0, 0],
         counts,
-        rulebook[0, 0],
+        rulebook.reshape(taps, 1, rows),
         face_rows[0, 0],
         gain_one[None],
         shift_one[None],

time: 37.1 us -> 31.9 us (0.86)
  Pallas kernels: 31.6 us -> 27.9 us
  local copies, waits for them, and re-layouts: 4.48 us -> 3.05 us
    pallas_call x1, Pallas kernels: 31.6 us -> 27.9 us  [per_device(): pl.pallas_call(partial(block_kernel, n_slab, n_tile), out_shape=jax.Shape...]
    unnamed x18 -> x15, local copies, waits for them, and re-layouts: 4.48 us -> 3.05 us
where the time goes in v2:
time: 31.9 us; the launch traced here: 31.6 us
  Pallas kernels  27.9 us (87%)
  local copies, waits for them, and re-layouts  3.05 us (10%)
  between operations  0.7 us (2%)
    pallas_call x1, Pallas kernels, per_device(): pl.pallas_call(partial(block_kernel, n_slab, n_tile), out_shape=jax.Shape...  27.9 us
    unnamed x15, local copies, waits for them, and re-layouts  3.05 us

profile of v2, /device:TPU:0, one launch (start us, length us, event | category | flops | bytes accessed | tf_op | source)
XLA Modules:
  0.0 31.6 jit_solution(3983321361185953475)
XLA Ops:
  0.7 0.0 copy-start.6
  0.7 0.0 copy-start.2
  0.7 0.0 copy-start.3
  0.7 0.0 copy-start.4
  0.7 0.0 copy-start.5
  0.7 0.6 %copy-done.6 = f32[128]{0:T(128)S(1)} copy-done((f32[128]{0:T(128)S(1)}, f32[128]{0:T(128)}, u32[]{:S(2)}) %copy-start.6) | copy-done | bytes 536
  1.3 0.0 copy-done.2
  1.4 0.0 copy-done.3
  1.4 0.0 copy-done.4
  1.4 0.0 copy-done.5
  1.4 0.0 copy-start
  1.4 0.9 %copy-done = bf16[1,1,512,128]{3,2,1,0:T(8,128)(2,1)S(1)} copy-done((bf16[1,1,512,128]{3,2,1,0:T(8,128)(2,1)S(1)}, bf16[1,1,512,128]{3,2,1,0:T(8,128)(2,1)}, u32[]{:S(2)}) %copy-start) | copy-done | bytes 131096
  2.3 0.0 copy-start.1
  2.3 0.8 %copy-done.1 = s32[1,1,27,512]{3,1,2,0:T(1,128)S(1)} copy-done((s32[1,1,27,512]{3,1,2,0:T(1,128)S(1)}, s32[1,1,27,512]{3,1,2,0:T(1,128)}, u32[]{:S(2)}) %copy-start.1) | copy-done | bytes 55320
  3.1 27.9 %shard_map.100 = bf16[512,128]{1,0:T(8,128)(2,1)S(1)} custom-call(bf16[512,128]{1,0:T(8,128)(2,1)S(1)} %bitcast.11, s32[1,1]{1,0:T(1,128)S(6)} %copy.12.count_ref, s32[27,1,512]{2,1,0:T(1,128)S(1)} %bitcast.12, s32[4,64]{1,0:T(4,128)S(1)} %bitcast.13, f32[1,128]{1,0:T(1,128)S(1)} %bitcast.14, f32[1,128]{1,0:T(1,128)S(1)} %bitcast.15, f32[1,128]{1,0:T(1,128)S(1)} %bitcast.16, ...), custom_call_target="tpu_custom_call" | custom-call | tf_op jit(solution)/shard_map/pallas_call | solution.py:327
  31.0 0.7 %copy.13 = bf16[1,1,512,128]{3,2,1,0:T(8,128)(2,1)} copy(bf16[1,1,512,128]{3,2,1,0:T(8,128)(2,1)S(1)} %bitcast.10) | data formatting | bytes 262144
Async XLA Ops:
  0.7 0.7 %copy-start.6 = (f32[128]{0:T(128)S(1)}, f32[128]{0:T(128)}, u32[]{:S(2)}) copy-start(f32[128]{0:T(128)} %param.19) | copy-start | bytes 1540
  0.7 0.7 %copy-start.2 = (s32[1,1,4,64]{3,2,1,0:T(4,128)S(1)}, s32[1,1,4,64]{3,2,1,0:T(4,128)}, u32[]{:S(2)}) copy-start(s32[1,1,4,64]{3,2,1,0:T(4,128)} %param.13) | copy-start | bytes 3076
  0.7 0.7 %copy-start.3 = (f32[128]{0:T(128)S(1)}, f32[128]{0:T(128)}, u32[]{:S(2)}) copy-start(f32[128]{0:T(128)} %param.15) | copy-start | bytes 1540
  0.7 0.7 %copy-start.4 = (f32[128]{0:T(128)S(1)}, f32[128]{0:T(128)}, u32[]{:S(2)}) copy-start(f32[128]{0:T(128)} %param.16) | copy-start | bytes 1540
  0.7 0.7 %copy-start.5 = (f32[128]{0:T(128)S(1)}, f32[128]{0:T(128)}, u32[]{:S(2)}) copy-start(f32[128]{0:T(128)} %param.18) | copy-start | bytes 1540
  1.4 0.9 %copy-start = (bf16[1,1,512,128]{3,2,1,0:T(8,128)(2,1)S(1)}, bf16[1,1,512,128]{3,2,1,0:T(8,128)(2,1)}, u32[]{:S(2)}) copy-start(bf16[1,1,512,128]{3,2,1,0:T(8,128)(2,1)} %param.10) | copy-start | bytes 393220
  2.3 0.8 %copy-start.1 = (s32[1,1,27,512]{3,1,2,0:T(1,128)S(1)}, s32[1,1,27,512]{3,1,2,0:T(1,128)}, u32[]{:S(2)}) copy-start(s32[1,1,27,512]{3,1,2,0:T(1,128)} %param.12) | copy-start | bytes 165892

commit v3 on v2

--- a/solution.py
+++ b/solution.py
@@ -39,16 +39,20 @@
     count_ref,
     rule_hbm,
     face_hbm,
-    gain_one_ref,
-    shift_one_ref,
-    gain_two_ref,
-    shift_two_ref,
+    gain_one_hbm,
+    shift_one_hbm,
+    gain_two_hbm,
+    shift_two_hbm,
     conv_one_ref,
     conv_two_ref,
     out_ref,
     feat_ref,
     rule_ref,
     face_ref,
+    gain_one_ref,
+    shift_one_ref,
+    gain_two_ref,
+    shift_two_ref,
     weight_ref,
     weight_t_ref,
     onehot_ref,
@@ -62,8 +66,8 @@
     lhs_ref,
     picked_ref,
     stats_ref,
+    counts_ref,
     input_sem,
-    weight_sem,
     send_sem,
     recv_sem,
     stat_send_sem,
@@ -76,38 +80,58 @@
     n_dev = n_slab * n_tile
     blocks = rows // BLOCK
     group = taps // 3
+    ahead = 2
     slab = lax.axis_index("slab")
     tile = lax.axis_index("tile")
     me = slab * n_tile + tile
 
+    def fetch(i, src, dst):
+        return pltpu.make_async_copy(src, dst, input_sem.at[i])
+
     input_copies = [
-        pltpu.make_async_copy(src, dst, input_sem.at[i])
-        for i, (src, dst) in enumerate(
-            ((feat_hbm, feat_ref), (face_hbm, face_ref), (rule_hbm, rule_ref))
-        )
+        fetch(0, feat_hbm, feat_ref),
+        fetch(1, face_hbm, face_ref),
+        fetch(2, rule_hbm, rule_ref),
     ]
-    for copy in input_copies:
-        copy.start()
+    affine_copies = [
+        fetch(3, gain_one_hbm, gain_one_ref),
+        fetch(4, shift_one_hbm, shift_one_ref),
+        fetch(5, gain_two_hbm, gain_two_ref),
+        fetch(6, shift_two_hbm, shift_two_ref),
+    ]
     weight_copies = [
-        pltpu.make_async_copy(src, weight_ref.at[i], weight_sem.at[i])
-        for i, src in enumerate((conv_one_ref, conv_two_ref))
+        fetch(7, conv_one_ref, weight_ref.at[0]),
+        fetch(8, conv_two_ref, weight_ref.at[1]),
     ]
-    for copy in weight_copies:
+    for copy in (input_copies[1], input_copies[0], input_copies[2]):
         copy.start()
     halo_ref[...] = jnp.zeros_like(halo_ref)
     wide_halo_ref[...] = jnp.zeros_like(wide_halo_ref)
 
-    def peer_of(step):
-        peer = lax.rem(me + step, n_dev)
-        return {"slab": peer // n_tile, "tile": lax.rem(peer, n_tile)}
+    def wrapped(place, step, size):
+        moved = place + step
+        return jnp.where(moved >= size, moved - size, moved)
+
+    def each_peer(act):
+        for j in range(n_tile):
+            other = tile if j == 0 else wrapped(tile, j, n_tile)
+
+            def visit(i, carry):
+                act({"slab": wrapped(slab, i, n_slab), "tile": other})
+                return carry
+
+            first = 1 if j == 0 else 0
+            lax.fori_loop(first, n_slab, visit, 0, unroll=n_slab <= 16)
 
     barrier = pltpu.get_barrier_semaphore()
 
-    def greet(step, carry):
-        pl.semaphore_signal(barrier, inc=1, device_id=peer_of(step), device_id_type=MESH)
-        return carry
-
-    lax.fori_loop(1, n_dev, greet, 0)
+    each_peer(
+        lambda peer: pl.semaphore_signal(
+            barrier, inc=1, device_id=peer, device_id_type=MESH
+        )
+    )
+    for copy in weight_copies + affine_copies:
+        copy.start()
 
     def halo(which, start):
         source, target = ((send_ref, halo_ref), (wide_send_ref, wide_halo_ref))[which]
@@ -172,12 +196,38 @@
         rule < rows, rule // BLOCK, jnp.where(rule < above + tile_len, blocks, blocks + 1)
     )
     part_ref[...] = part
-    position = lax.broadcasted_iota(jnp.int32, (BLOCK, rows), 0)
+    position = lax.broadcasted_iota(jnp.int32, (BLOCK, rows), 0).astype(F32).astype(BF16)
+    place = place.astype(F32).astype(BF16)
+    one, none = jnp.ones((BLOCK, rows), BF16), jnp.zeros((BLOCK, rows), BF16)
     for k in range(taps):
-        onehot_ref[k] = jnp.where(position == place[k], 1.0, 0.0).astype(BF16)
-
+        onehot_ref[k] = jnp.where(position == place[k], one, none)
+
+    count = count_ref[0, 0]
+    live = (lax.broadcasted_iota(jnp.int32, (rows, 1), 0) < count).astype(F32)
+
+    def share(which, buffer):
+        mine = buffer.at[me]
+        each_peer(
+            lambda peer: pltpu.make_async_remote_copy(
+                src_ref=mine,
+                dst_ref=mine,
+                send_sem=stat_send_sem.at[which],
+                recv_sem=stat_recv_sem.at[which],
+                device_id=peer,
+                device_id_type=MESH,
+            ).start()
+        )
+
+    def shared(which, buffer):
+        others = buffer.at[pl.ds(0, n_dev - 1)]
+        pltpu.make_async_copy(others, others, stat_recv_sem.at[which]).wait()
+        pltpu.make_async_copy(others, others, stat_send_sem.at[which]).wait()
+        return jnp.sum(buffer[...], axis=0)
+
+    counts_ref[me] = jnp.full((1, channels), count.astype(F32))
     pl.semaphore_wait(barrier, n_dev - 1)
     halo(0, True)
+    share(2, counts_ref)
 
     def load_local(values):
         for b in range(blocks):
@@ -194,26 +244,30 @@
             lhs_ref[y, low:, half:] = jnp.zeros_like(turned[0]) if other is None else other
 
     load_local(feat)
-    for i in range(2):
+    def turn_weights(i):
         weight_copies[i].wait()
         for x in range(3):
             weight_t_ref[i, x] = weight_ref[i, x * group * channels : (x + 1) * group * channels, :].T
+
+    turn_weights(0)
 
     def choose(home, found, value, chosen):
         for i, b in enumerate(chosen):
             value = jnp.where(home == b, found[i * channels : (i + 1) * channels], value)
         return value
 
-    def pick_local(tap, carry):
-        found = jnp.dot(
-            lhs_ref[0, 0 : blocks * channels], onehot_ref[tap], preferred_element_type=F32
-        )
-        value = choose(part_ref[tap], found, jnp.zeros((channels, rows), F32), range(blocks))
-        picked_ref[tap] = value.astype(BF16)
+    def pick_local(x, carry):
+        for j in range(group):
+            tap = x * group + j
+            found = jnp.dot(
+                lhs_ref[0, 0 : blocks * channels], onehot_ref[tap], preferred_element_type=F32
+            )
+            value = choose(part_ref[tap], found, jnp.zeros((channels, rows), F32), range(blocks))
+            picked_ref[tap] = value.astype(BF16)
         return carry
 
     def convolve(which, picked):
-        def one(x, total):
+        def add_group(x, total):
             for j in range(group):
                 tap = x * group + j
                 home = part_ref[tap]
@@ -235,20 +289,7 @@
             taken = picked_ref[pl.ds(x * group, group)].reshape(group * channels, rows)
             return total + jnp.dot(weight_t_ref[which, x], taken, preferred_element_type=F32)
 
-        return lax.fori_loop(0, 3, one, jnp.zeros((channels, rows), F32))
-
-    count = count_ref[0, 0]
-    live = (lax.broadcasted_iota(jnp.int32, (rows, 1), 0) < count).astype(F32)
-
-    def stat_copy(which, target):
-        return pltpu.make_async_remote_copy(
-            src_ref=stats_ref.at[which, me],
-            dst_ref=stats_ref.at[which, me],
-            send_sem=stat_send_sem.at[which],
-            recv_sem=stat_recv_sem.at[which],
-            device_id=target,
-            device_id_type=MESH,
-        )
+        return add_group
 
     def tell_sums(which, values):
         kept = values * live
@@ -256,31 +297,24 @@
             [
                 jnp.sum(kept, axis=0, keepdims=True),
                 jnp.sum(kept * values, axis=0, keepdims=True),
-                jnp.full((2, channels), count.astype(F32)),
             ],
             axis=0,
         )
-
-        def tell(step, carry):
-            stat_copy(which, peer_of(step)).start()
-            return carry
-
-        lax.fori_loop(1, n_dev, tell, 0)
-
-    def affine(which, gain_ref, shift_ref):
-        others = stats_ref.at[which, pl.ds(0, n_dev - 1)]
-        pltpu.make_async_copy(others, others, stat_recv_sem.at[which]).wait()
-        pltpu.make_async_copy(others, others, stat_send_sem.at[which]).wait()
-        total = jnp.sum(stats_ref[which], axis=0)
-        average = total[0:1] / total[2:3]
-        variance = total[1:2] / total[2:3] - average * average
+        share(which, stats_ref.at[which])
+
+    def affine(which, voxels, gain_ref, shift_ref):
+        total = shared(which, stats_ref.at[which])
+        average = total[0:1] / voxels
+        variance = total[1:2] / voxels - average * average
         scale = lax.rsqrt(variance + EPSILON) * gain_ref[...]
         return lambda values: (values - average) * scale + shift_ref[...]
 
-    lax.fori_loop(0, taps, pick_local, 0, unroll=3)
+    lax.fori_loop(0, ahead, pick_local, 0)
     halo(0, False)
     load_halo([halo_ref[i] for i in range(3)])
-    first = convolve(0, True).T
+    blank = jnp.zeros((channels, rows), F32)
+    first = lax.fori_loop(0, ahead, convolve(0, True), blank)
+    first = lax.fori_loop(ahead, 3, convolve(0, False), first).T
     tell_sums(0, first)
     coarse = first.astype(BF16)
     fine = (first - coarse.astype(F32)).astype(BF16)
@@ -291,13 +325,17 @@
     )
     wide_send_ref[...] = both[:, 0:channels] + both[:, channels:]
     halo(1, True)
-    norm_one = affine(0, gain_one_ref, shift_one_ref)
+    turn_weights(1)
+    for copy in affine_copies:
+        copy.wait()
+    voxels = shared(2, counts_ref)
+    norm_one = affine(0, voxels, gain_one_ref, shift_one_ref)
     load_local((live * jnp.maximum(norm_one(first), 0.0)).astype(BF16))
     halo(1, False)
     load_halo([jnp.maximum(norm_one(wide_halo_ref[i]), 0.0).astype(BF16) for i in range(3)])
-    second = convolve(1, False).T
+    second = lax.fori_loop(0, 3, convolve(1, False), blank).T
     tell_sums(1, second)
-    norm_two = affine(1, gain_two_ref, shift_two_ref)
+    norm_two = affine(1, voxels, gain_two_ref, shift_two_ref)
     summed = norm_two(second) + feat_ref[...].astype(F32)
     out_ref[...] = (live * jnp.maximum(summed, 0.0)).astype(BF16)
 
@@ -327,12 +365,16 @@
     output = pl.pallas_call(
         partial(block_kernel, n_slab, n_tile),
         out_shape=jax.ShapeDtypeStruct((rows, channels), features.dtype),
-        in_specs=[hbm, smem, hbm, hbm, vmem, vmem, vmem, vmem, hbm, hbm],
+        in_specs=[hbm, smem] + [hbm] * 8,
         out_specs=vmem,
         scratch_shapes=[
             pltpu.VMEM((rows, channels), BF16),
             pltpu.VMEM((taps, 1, rows), jnp.int32),
             pltpu.VMEM((faces, face_len), jnp.int32),
+            pltpu.VMEM((1, channels), F32),
+            pltpu.VMEM((1, channels), F32),
+            pltpu.VMEM((1, channels), F32),
+            pltpu.VMEM((1, channels), F32),
             pltpu.VMEM((2, taps * channels, channels), BF16),
             pltpu.VMEM((2, 3, channels, group), BF16),
             pltpu.VMEM((taps, BLOCK, rows), BF16),
@@ -345,16 +387,16 @@
             pltpu.VMEM((3, BLOCK // 2, channels), F32),
             pltpu.VMEM((3, (blocks + 1) * channels, BLOCK), BF16),
             pltpu.VMEM((taps, channels, rows), BF16),
-            pltpu.VMEM((2, n_slab * n_tile, 4, channels), F32),
-            pltpu.SemaphoreType.DMA((3,)),
-            pltpu.SemaphoreType.DMA((2,)),
+            pltpu.VMEM((2, n_slab * n_tile, 2, channels), F32),
+            pltpu.VMEM((n_slab * n_tile, 1, channels), F32),
+            pltpu.SemaphoreType.DMA((9,)),
             pltpu.SemaphoreType.DMA((2, 8)),
             pltpu.SemaphoreType.DMA((2, 8)),
-            pltpu.SemaphoreType.DMA((2,)),
-            pltpu.SemaphoreType.DMA((2,)),
+            pltpu.SemaphoreType.DMA((3,)),
+            pltpu.SemaphoreType.DMA((3,)),
         ],
         compiler_params=pltpu.CompilerParams(
-            collective_id=0, has_side_effects=True, vmem_limit_bytes=55500000
+            collective_id=0, has_side_effects=True, vmem_limit_bytes=63200000
         ),
     )(
         features[0, 0],

time: 31.9 us -> 29.5 us (0.925)
  local copies, waits for them, and re-layouts: 3.05 us -> 1.57 us
  Pallas kernels: 27.9 us -> 27.1 us
    unnamed x15 -> x1, local copies, waits for them, and re-layouts: 3.05 us -> 1.57 us
    pallas_call x1, Pallas kernels: 27.9 us -> 27.1 us  [per_device(): pl.pallas_call(partial(block_kernel, n_slab, n_tile), out_shape=jax.Shape...]
where the time goes in v3:
time: 29.5 us; the launch traced here: 29.3 us
  Pallas kernels  27.1 us (92%)
  local copies, waits for them, and re-layouts  1.57 us (5%)
  between operations  0.66 us (2%)
    pallas_call x1, Pallas kernels, per_device(): pl.pallas_call(partial(block_kernel, n_slab, n_tile), out_shape=jax.Shape...  27.1 us
    unnamed x1, local copies, waits for them, and re-layouts  1.57 us

profile of v3, /device:TPU:0, one launch (start us, length us, event | category | flops | bytes accessed | tf_op | source)
XLA Modules:
  0.0 29.3 jit_solution(2524308989848420019)
XLA Ops:
  0.7 27.1 %shard_map.100 = bf16[512,128]{1,0:T(8,128)(2,1)} custom-call(bf16[512,128]{1,0:T(8,128)(2,1)} %bitcast.13, s32[1,1]{1,0:T(1,128)S(6)} %copy.12.count_ref, s32[27,1,512]{2,1,0:T(1,128)} %bitcast.14, s32[4,64]{1,0:T(4,128)} %bitcast.15, f32[1,128]{1,0:T(1,128)} %bitcast.16, f32[1,128]{1,0:T(1,128)} %bitcast.17, f32[1,128]{1,0:T(1,128)} %bitcast.18, ...), custom_call_target="tpu_custom_call" | custom-call | tf_op jit(solution)/shard_map/pallas_call | solution.py:365
  27.7 1.6 %copy.13 = bf16[1,1,512,128]{3,2,1,0:T(8,128)(2,1)} copy(bf16[1,1,512,128]{3,2,1,0:T(8,128)(2,1)} %bitcast.12) | data formatting | bytes 262144

commit v4 on v3

--- a/solution.py
+++ b/solution.py
@@ -57,8 +57,10 @@
     weight_t_ref,
     onehot_ref,
     part_ref,
+    keep_ref,
     face_hot_ref,
     square_ref,
+    slope_ref,
     send_ref,
     wide_send_ref,
     halo_ref,
@@ -80,7 +82,6 @@
     n_dev = n_slab * n_tile
     blocks = rows // BLOCK
     group = taps // 3
-    ahead = 2
     slab = lax.axis_index("slab")
     tile = lax.axis_index("tile")
     me = slab * n_tile + tile
@@ -108,20 +109,22 @@
     halo_ref[...] = jnp.zeros_like(halo_ref)
     wide_halo_ref[...] = jnp.zeros_like(wide_halo_ref)
 
-    def wrapped(place, step, size):
-        moved = place + step
-        return jnp.where(moved >= size, moved - size, moved)
+    def moved(place, step, size):
+        if size & (size - 1) == 0:
+            return place ^ step
+        place = place + step
+        return jnp.where(place >= size, place - size, place)
 
     def each_peer(act):
-        for j in range(n_tile):
-            other = tile if j == 0 else wrapped(tile, j, n_tile)
+        for j in reversed(range(n_tile)):
+            other = moved(tile, j, n_tile) if j else tile
 
             def visit(i, carry):
-                act({"slab": wrapped(slab, i, n_slab), "tile": other})
+                act({"slab": moved(slab, n_slab - 1 - i, n_slab), "tile": other})
                 return carry
 
-            first = 1 if j == 0 else 0
-            lax.fori_loop(first, n_slab, visit, 0, unroll=n_slab <= 16)
+            last = n_slab if j else n_slab - 1
+            lax.fori_loop(0, last, visit, 0, unroll=n_slab <= 16)
 
     barrier = pltpu.get_barrier_semaphore()
 
@@ -196,6 +199,8 @@
         rule < rows, rule // BLOCK, jnp.where(rule < above + tile_len, blocks, blocks + 1)
     )
     part_ref[...] = part
+    dead = (part > blocks) | ((rule < rows) & (rule >= count_ref[0, 0]))
+    keep_ref[...] = jnp.where(dead, 0, 1)
     position = lax.broadcasted_iota(jnp.int32, (BLOCK, rows), 0).astype(F32).astype(BF16)
     place = place.astype(F32).astype(BF16)
     one, none = jnp.ones((BLOCK, rows), BF16), jnp.zeros((BLOCK, rows), BF16)
@@ -266,30 +271,25 @@
             picked_ref[tap] = value.astype(BF16)
         return carry
 
-    def convolve(which, picked):
-        def add_group(x, total):
-            for j in range(group):
-                tap = x * group + j
-                home = part_ref[tap]
-                if picked:
-                    found = jnp.dot(
-                        lhs_ref[j // 3, blocks * channels :],
-                        onehot_ref[tap],
-                        preferred_element_type=F32,
-                    )
-                    value = choose(home, found, picked_ref[tap].astype(F32), (blocks,))
-                else:
-                    found = jnp.dot(
-                        lhs_ref[j // 3], onehot_ref[tap], preferred_element_type=F32
-                    )
-                    value = choose(
-                        home, found, jnp.zeros((channels, rows), F32), range(blocks + 1)
-                    )
-                picked_ref[tap] = value.astype(BF16)
-            taken = picked_ref[pl.ds(x * group, group)].reshape(group * channels, rows)
-            return total + jnp.dot(weight_t_ref[which, x], taken, preferred_element_type=F32)
-
-        return add_group
+    def pick_halo(tap, j):
+        found = jnp.dot(
+            lhs_ref[j // 3, blocks * channels :], onehot_ref[tap], preferred_element_type=F32
+        )
+        value = choose(part_ref[tap], found, picked_ref[tap].astype(F32), (blocks,))
+        picked_ref[tap] = value.astype(BF16)
+
+    def pick_halos(x, carry):
+        for j in range(group):
+            pick_halo(x * group + j, j)
+        return carry
+
+    def multiply(which, x, total):
+        taken = picked_ref[pl.ds(x * group, group)].reshape(group * channels, rows)
+        return total + jnp.dot(weight_t_ref[which, x], taken, preferred_element_type=F32)
+
+    def convolve_one(x, total):
+        pick_halos(x, 0)
+        return multiply(0, x, total)
 
     def tell_sums(which, values):
         kept = values * live
@@ -301,21 +301,21 @@
             axis=0,
         )
         share(which, stats_ref.at[which])
+        return stats_ref[which, me][0:1] / count.astype(F32)
 
     def affine(which, voxels, gain_ref, shift_ref):
         total = shared(which, stats_ref.at[which])
         average = total[0:1] / voxels
         variance = total[1:2] / voxels - average * average
         scale = lax.rsqrt(variance + EPSILON) * gain_ref[...]
-        return lambda values: (values - average) * scale + shift_ref[...]
-
-    lax.fori_loop(0, ahead, pick_local, 0)
+        return scale, shift_ref[...] - average * scale
+
+    lax.fori_loop(0, 3, pick_local, 0)
     halo(0, False)
     load_halo([halo_ref[i] for i in range(3)])
     blank = jnp.zeros((channels, rows), F32)
-    first = lax.fori_loop(0, ahead, convolve(0, True), blank)
-    first = lax.fori_loop(ahead, 3, convolve(0, False), first).T
-    tell_sums(0, first)
+    first = lax.fori_loop(0, 3, convolve_one, blank).T
+    centre = tell_sums(0, first)
     coarse = first.astype(BF16)
     fine = (first - coarse.astype(F32)).astype(BF16)
     both = jnp.dot(
@@ -325,18 +325,34 @@
     )
     wide_send_ref[...] = both[:, 0:channels] + both[:, channels:]
     halo(1, True)
+    load_local((first - centre).astype(BF16))
+    lax.fori_loop(0, 3, pick_local, 0)
+    halo(1, False)
+    load_halo([(wide_halo_ref[i] - centre).astype(BF16) for i in range(3)])
+    lax.fori_loop(0, 3, pick_halos, 0)
     turn_weights(1)
     for copy in affine_copies:
         copy.wait()
     voxels = shared(2, counts_ref)
-    norm_one = affine(0, voxels, gain_one_ref, shift_one_ref)
-    load_local((live * jnp.maximum(norm_one(first), 0.0)).astype(BF16))
-    halo(1, False)
-    load_halo([jnp.maximum(norm_one(wide_halo_ref[i]), 0.0).astype(BF16) for i in range(3)])
-    second = lax.fori_loop(0, 3, convolve(1, False), blank).T
+    scale, offset = affine(0, voxels, gain_one_ref, shift_one_ref)
+
+    square_ref[...] = jnp.broadcast_to(scale, (channels, channels)).T
+    slope_ref[...] = jnp.broadcast_to(centre * scale + offset, (channels, channels)).T
+
+    def convolve_two(x, total):
+        slope = jnp.concatenate([square_ref[...]] * (rows // channels), axis=1)
+        level = jnp.concatenate([slope_ref[...]] * (rows // channels), axis=1)
+        for j in range(group):
+            tap = x * group + j
+            value = jnp.maximum(picked_ref[tap].astype(F32) * slope + level, 0.0)
+            value = jnp.where(keep_ref[tap] > 0, value, 0.0)
+            picked_ref[tap] = value.astype(BF16)
+        return multiply(1, x, total)
+
+    second = lax.fori_loop(0, 3, convolve_two, blank).T
     tell_sums(1, second)
-    norm_two = affine(1, voxels, gain_two_ref, shift_two_ref)
-    summed = norm_two(second) + feat_ref[...].astype(F32)
+    scale, offset = affine(1, voxels, gain_two_ref, shift_two_ref)
+    summed = second * scale + offset + feat_ref[...].astype(F32)
     out_ref[...] = (live * jnp.maximum(summed, 0.0)).astype(BF16)
 
 
@@ -379,8 +395,10 @@
             pltpu.VMEM((2, 3, channels, group), BF16),
             pltpu.VMEM((taps, BLOCK, rows), BF16),
             pltpu.VMEM((taps, 1, rows), jnp.int32),
+            pltpu.VMEM((taps, 1, rows), jnp.int32),
             pltpu.VMEM((faces * face_len, rows), BF16),
-            pltpu.VMEM((128, 128), F32),
+            pltpu.VMEM((channels, channels), F32),
+            pltpu.VMEM((channels, channels), F32),
             pltpu.VMEM((faces * face_len, channels), BF16),
             pltpu.VMEM((faces * face_len, channels), F32),
             pltpu.VMEM((3, BLOCK // 2, channels), BF16),

time: 29.5 us -> 27.9 us (0.946)
  Pallas kernels: 27.1 us -> 25.5 us
    pallas_call x1, Pallas kernels: 27.1 us -> 25.5 us  [per_device(): pl.pallas_call(partial(block_kernel, n_slab, n_tile), out_shape=jax.Shape...]
where the time goes in v4:
time: 27.9 us; the launch traced here: 27.8 us
  Pallas kernels  25.5 us (91%)
  local copies, waits for them, and re-layouts  1.57 us (6%)
  between operations  0.66 us (2%)
    pallas_call x1, Pallas kernels, per_device(): pl.pallas_call(partial(block_kernel, n_slab, n_tile), out_shape=jax.Shape...  25.5 us
    unnamed x1, local copies, waits for them, and re-layouts  1.57 us

profile of v4, /device:TPU:0, one launch (start us, length us, event | category | flops | bytes accessed | tf_op | source)
XLA Modules:
  0.0 27.8 jit_solution(15015402292930006378)
XLA Ops:
  0.7 25.5 %shard_map.100 = bf16[512,128]{1,0:T(8,128)(2,1)} custom-call(bf16[512,128]{1,0:T(8,128)(2,1)} %bitcast.13, s32[1,1]{1,0:T(1,128)S(6)} %copy.12.count_ref, s32[27,1,512]{2,1,0:T(1,128)} %bitcast.14, s32[4,64]{1,0:T(4,128)} %bitcast.15, f32[1,128]{1,0:T(1,128)} %bitcast.16, f32[1,128]{1,0:T(1,128)} %bitcast.17, f32[1,128]{1,0:T(1,128)} %bitcast.18, ...), custom_call_target="tpu_custom_call" | custom-call | tf_op jit(solution)/shard_map/pallas_call | solution.py:381
  26.2 1.6 %copy.13 = bf16[1,1,512,128]{3,2,1,0:T(8,128)(2,1)} copy(bf16[1,1,512,128]{3,2,1,0:T(8,128)(2,1)} %bitcast.12) | data formatting | bytes 262144

commit v5 on v4

--- a/solution.py
+++ b/solution.py
@@ -61,6 +61,7 @@
     face_hot_ref,
     square_ref,
     slope_ref,
+    own_ref,
     send_ref,
     wide_send_ref,
     halo_ref,
@@ -271,24 +272,21 @@
             picked_ref[tap] = value.astype(BF16)
         return carry
 
-    def pick_halo(tap, j):
-        found = jnp.dot(
-            lhs_ref[j // 3, blocks * channels :], onehot_ref[tap], preferred_element_type=F32
-        )
-        value = choose(part_ref[tap], found, picked_ref[tap].astype(F32), (blocks,))
-        picked_ref[tap] = value.astype(BF16)
-
-    def pick_halos(x, carry):
+    def pick_halos(x):
         for j in range(group):
-            pick_halo(x * group + j, j)
-        return carry
+            tap = x * group + j
+            found = jnp.dot(
+                lhs_ref[j // 3, blocks * channels :], onehot_ref[tap], preferred_element_type=F32
+            )
+            value = choose(part_ref[tap], found, picked_ref[tap].astype(F32), (blocks,))
+            picked_ref[tap] = value.astype(BF16)
 
     def multiply(which, x, total):
         taken = picked_ref[pl.ds(x * group, group)].reshape(group * channels, rows)
         return total + jnp.dot(weight_t_ref[which, x], taken, preferred_element_type=F32)
 
     def convolve_one(x, total):
-        pick_halos(x, 0)
+        pick_halos(x)
         return multiply(0, x, total)
 
     def tell_sums(which, values):
@@ -325,17 +323,25 @@
     )
     wide_send_ref[...] = both[:, 0:channels] + both[:, channels:]
     halo(1, True)
-    load_local((first - centre).astype(BF16))
+    centred = first - centre
+    for b in range(blocks):
+        turned = centred[b * BLOCK : (b + 1) * BLOCK].T
+        own_ref[:, b * BLOCK : (b + 1) * BLOCK] = turned
+        lhs_ref[0, b * channels : (b + 1) * channels, :] = turned.astype(BF16)
     lax.fori_loop(0, 3, pick_local, 0)
-    halo(1, False)
-    load_halo([(wide_halo_ref[i] - centre).astype(BF16) for i in range(3)])
-    lax.fori_loop(0, 3, pick_halos, 0)
     turn_weights(1)
     for copy in affine_copies:
         copy.wait()
     voxels = shared(2, counts_ref)
     scale, offset = affine(0, voxels, gain_one_ref, shift_one_ref)
 
+    halo(1, False)
+    load_halo(
+        [
+            jnp.maximum(wide_halo_ref[i] * scale + offset, 0.0).astype(BF16)
+            for i in range(3)
+        ]
+    )
     square_ref[...] = jnp.broadcast_to(scale, (channels, channels)).T
     slope_ref[...] = jnp.broadcast_to(centre * scale + offset, (channels, channels)).T
 
@@ -344,7 +350,15 @@
         level = jnp.concatenate([slope_ref[...]] * (rows // channels), axis=1)
         for j in range(group):
             tap = x * group + j
-            value = jnp.maximum(picked_ref[tap].astype(F32) * slope + level, 0.0)
+            value = picked_ref[tap].astype(F32)
+            if j == group // 2:
+                middle = jnp.full((channels, rows), x, jnp.int32) == 1
+                value = jnp.where(middle, own_ref[...], value)
+            value = jnp.maximum(value * slope + level, 0.0)
+            found = jnp.dot(
+                lhs_ref[j // 3, blocks * channels :], onehot_ref[tap], preferred_element_type=F32
+            )
+            value = choose(part_ref[tap], found, value, (blocks,))
             value = jnp.where(keep_ref[tap] > 0, value, 0.0)
             picked_ref[tap] = value.astype(BF16)
         return multiply(1, x, total)
@@ -399,6 +413,7 @@
             pltpu.VMEM((faces * face_len, rows), BF16),
             pltpu.VMEM((channels, channels), F32),
             pltpu.VMEM((channels, channels), F32),
+            pltpu.VMEM((channels, rows), F32),
             pltpu.VMEM((faces * face_len, channels), BF16),
             pltpu.VMEM((faces * face_len, channels), F32),
             pltpu.VMEM((3, BLOCK // 2, channels), BF16),

time: 27.9 us -> 28.3 us (1.014)
  Pallas kernels: 25.5 us -> 25.9 us
    pallas_call x1, Pallas kernels: 25.5 us -> 25.9 us  [per_device(): pl.pallas_call(partial(block_kernel, n_slab, n_tile), out_shape=jax.Shape...]
where the time goes in v5:
time: 28.3 us; the launch traced here: 28.1 us
  Pallas kernels  25.9 us (92%)
  local copies, waits for them, and re-layouts  1.57 us (6%)
  between operations  0.66 us (2%)
    pallas_call x1, Pallas kernels, per_device(): pl.pallas_call(partial(block_kernel, n_slab, n_tile), out_shape=jax.Shape...  25.9 us
    unnamed x1, local copies, waits for them, and re-layouts  1.57 us

profile of v5, /device:TPU:0, one launch (start us, length us, event | category | flops | bytes accessed | tf_op | source)
XLA Modules:
  0.0 28.1 jit_solution(10122829991242845876)
XLA Ops:
  0.7 25.9 %shard_map.100 = bf16[512,128]{1,0:T(8,128)(2,1)} custom-call(bf16[512,128]{1,0:T(8,128)(2,1)} %bitcast.13, s32[1,1]{1,0:T(1,128)S(6)} %copy.12.count_ref, s32[27,1,512]{2,1,0:T(1,128)} %bitcast.14, s32[4,64]{1,0:T(4,128)} %bitcast.15, f32[1,128]{1,0:T(1,128)} %bitcast.16, f32[1,128]{1,0:T(1,128)} %bitcast.17, f32[1,128]{1,0:T(1,128)} %bitcast.18, ...), custom_call_target="tpu_custom_call" | custom-call | tf_op jit(solution)/shard_map/pallas_call | solution.py:395
  26.6 1.6 %copy.13 = bf16[1,1,512,128]{3,2,1,0:T(8,128)(2,1)} copy(bf16[1,1,512,128]{3,2,1,0:T(8,128)(2,1)} %bitcast.12) | data formatting | bytes 262144

commit v6 on v4

--- a/solution.py
+++ b/solution.py
@@ -61,6 +61,7 @@
     face_hot_ref,
     square_ref,
     slope_ref,
+    own_ref,
     send_ref,
     wide_send_ref,
     halo_ref,
@@ -278,18 +279,14 @@
         value = choose(part_ref[tap], found, picked_ref[tap].astype(F32), (blocks,))
         picked_ref[tap] = value.astype(BF16)
 
-    def pick_halos(x, carry):
+    def pick_halos(x):
         for j in range(group):
-            pick_halo(x * group + j, j)
-        return carry
+            if x != 1 or j // 3 != 1:
+                pick_halo(x * group + j, j)
 
     def multiply(which, x, total):
         taken = picked_ref[pl.ds(x * group, group)].reshape(group * channels, rows)
         return total + jnp.dot(weight_t_ref[which, x], taken, preferred_element_type=F32)
-
-    def convolve_one(x, total):
-        pick_halos(x, 0)
-        return multiply(0, x, total)
 
     def tell_sums(which, values):
         kept = values * live
@@ -314,7 +311,11 @@
     halo(0, False)
     load_halo([halo_ref[i] for i in range(3)])
     blank = jnp.zeros((channels, rows), F32)
-    first = lax.fori_loop(0, 3, convolve_one, blank).T
+    first = blank
+    for x in range(3):
+        pick_halos(x)
+        first = multiply(0, x, first)
+    first = first.T
     centre = tell_sums(0, first)
     coarse = first.astype(BF16)
     fine = (first - coarse.astype(F32)).astype(BF16)
@@ -325,12 +326,17 @@
     )
     wide_send_ref[...] = both[:, 0:channels] + both[:, channels:]
     halo(1, True)
-    load_local((first - centre).astype(BF16))
+    centred = first - centre
+    for b in range(blocks):
+        turned = centred[b * BLOCK : (b + 1) * BLOCK].T
+        own_ref[:, b * BLOCK : (b + 1) * BLOCK] = turned
+        lhs_ref[0, b * channels : (b + 1) * channels, :] = turned.astype(BF16)
     lax.fori_loop(0, 3, pick_local, 0)
+    turn_weights(1)
     halo(1, False)
     load_halo([(wide_halo_ref[i] - centre).astype(BF16) for i in range(3)])
-    lax.fori_loop(0, 3, pick_halos, 0)
-    turn_weights(1)
+    for x in range(3):
+        pick_halos(x)
     for copy in affine_copies:
         copy.wait()
     voxels = shared(2, counts_ref)
@@ -344,7 +350,11 @@
         level = jnp.concatenate([slope_ref[...]] * (rows // channels), axis=1)
         for j in range(group):
             tap = x * group + j
-            value = jnp.maximum(picked_ref[tap].astype(F32) * slope + level, 0.0)
+            value = picked_ref[tap].astype(F32)
+            if j == group // 2:
+                middle = jnp.full((channels, rows), x, jnp.int32) == 1
+                value = jnp.where(middle, own_ref[...], value)
+            value = jnp.maximum(value * slope + level, 0.0)
             value = jnp.where(keep_ref[tap] > 0, value, 0.0)
             picked_ref[tap] = value.astype(BF16)
         return multiply(1, x, total)
@@ -399,6 +409,7 @@
             pltpu.VMEM((faces * face_len, rows), BF16),
             pltpu.VMEM((channels, channels), F32),
             pltpu.VMEM((channels, channels), F32),
+            pltpu.VMEM((channels, rows), F32),
             pltpu.VMEM((faces * face_len, channels), BF16),
             pltpu.VMEM((faces * face_len, channels), F32),
             pltpu.VMEM((3, BLOCK // 2, channels), BF16),

time: 27.9 us -> 26.5 us (0.950)
  Pallas kernels: 25.5 us -> 24.1 us
    pallas_call x1, Pallas kernels: 25.5 us -> 24.1 us  [per_device(): pl.pallas_call(partial(block_kernel, n_slab, n_tile), out_shape=jax.Shape...]
where the time goes in v6:
time: 26.5 us; the launch traced here: 26.3 us
  Pallas kernels  24.1 us (91%)
  local copies, waits for them, and re-layouts  1.57 us (6%)
  between operations  0.66 us (2%)
    pallas_call x1, Pallas kernels, per_device(): pl.pallas_call(partial(block_kernel, n_slab, n_tile), out_shape=jax.Shape...  24.1 us
    unnamed x1, local copies, waits for them, and re-layouts  1.57 us

profile of v6, /device:TPU:0, one launch (start us, length us, event | category | flops | bytes accessed | tf_op | source)
XLA Modules:
  0.0 26.3 jit_solution(12150368653012623674)
XLA Ops:
  0.7 24.1 %shard_map.100 = bf16[512,128]{1,0:T(8,128)(2,1)} custom-call(bf16[512,128]{1,0:T(8,128)(2,1)} %bitcast.13, s32[1,1]{1,0:T(1,128)S(6)} %copy.12.count_ref, s32[27,1,512]{2,1,0:T(1,128)} %bitcast.14, s32[4,64]{1,0:T(4,128)} %bitcast.15, f32[1,128]{1,0:T(1,128)} %bitcast.16, f32[1,128]{1,0:T(1,128)} %bitcast.17, f32[1,128]{1,0:T(1,128)} %bitcast.18, ...), custom_call_target="tpu_custom_call" | custom-call | tf_op jit(solution)/shard_map/pallas_call | solution.py:391
  24.8 1.6 %copy.13 = bf16[1,1,512,128]{3,2,1,0:T(8,128)(2,1)} copy(bf16[1,1,512,128]{3,2,1,0:T(8,128)(2,1)} %bitcast.12) | data formatting | bytes 262144
